TPU v7x, 32 devices: a whole 2x2x4 slice. The times are simulated.
32 devices in a mesh: grp: 2 (over x), seq: 8 (over z, y), tp: 2 (over core).
Axes of the slice: x: 2, y: 2, z: 4, core: 2. Of those that a mesh axis runs over, the one named last changes fastest.
Arguments:
- visual_q: bfloat16 [4096, 1536], P(('grp', 'seq'), 'tp'), parts along dimension 0, may hold values from -8 to 8
- visual_key_input: bfloat16 [4096, 1536], P(('grp', 'seq'), 'tp'), parts along dimension 0, may hold values from -8 to 8
- visual_v: bfloat16 [4096, 1536], P(('grp', 'seq'), 'tp'), parts along dimension 0, may hold values from -6 to 6
- text_k: bfloat16 [512, 1536], P(('grp', 'seq'), 'tp'), parts along dimension 0, may hold values from -6 to 6
- text_v: bfloat16 [512, 1536], P(('grp', 'seq'), 'tp'), parts along dimension 0, may hold values from -6 to 6
- text_mask: int32 [512], P(('grp', 'seq')), parts along dimension 0, may hold values from 0 to 1, as said below
- slab_order: int32 [16], P(('grp', 'seq')), parts along dimension 0, may hold values from 0 to 7, each once
- q_gain: float32 [128], replicated, may hold values from 0.8 to 6
- key_norm_gain: float32 [128], replicated, may hold values from 0.8 to 6
- w_out: bfloat16 [1536, 3072], P('tp'), may hold values from -0.8984375 to 0.8984375
Outputs:
- attended: bfloat16 [4096, 3072], P(('grp', 'seq', 'tp')), parts along dimension 0
There are 2 independent parts, one for each index of `grp`. A program takes and returns all parts, laid end to end along the dimension named above; an argument that names none is the same for every part. Nothing has to cross between parts.
Inputs may be any that keep to these rules, and one draw needn't show every extreme that they name: `text_mask`: the first entries are 1 and the rest 0, with at least 32 ones. `slab_order`: each slab number once.
All inputs are finite; a program needn't handle non-finite values.
Results may differ from a plain program's by a relative error of at most 0.013.
The roundings to bfloat16 on the way count: a program that leaves them out, or rounds other values in their place, can miss the bound.
Values may be sent and summed in bfloat16 or wider, within the bound.
A program may use at most 128 MiB of HBM per device.

v0:
```python
import functools

import jax
import jax.numpy as jnp
import numpy as np
from jax import lax
from jax.experimental import pallas as pl
from jax.experimental.pallas import tpu as pltpu
from jax.sharding import PartitionSpec as P

SLAB_H = 2
WIDE = 32
HEAD = 128
PARTS = (32, 48, 48)
NEGATIVE = -1e30
MESH = pl.DeviceIdType.MESH
F32 = jnp.float32
BF16 = jnp.bfloat16
LEAD_Y, LEAD_Z, LEAD_Q = 2, 2, 2
GROUP = 4


def lane_constants():
    lanes = np.zeros((8, HEAD), np.float32)
    perm = np.zeros((HEAD, HEAD), np.float32)
    offset = 0
    for index, size in enumerate(PARTS):
        half = size // 2
        f = np.float32(10000.0) ** (-np.arange(half, dtype=np.float32) / np.float32(half))
        lanes[0, offset : offset + half] = f
        lanes[0, offset + half : offset + size] = f
        lanes[1, offset : offset + size] = index
        lanes[2, offset : offset + half] = 1.0
        for j in range(half):
            perm[offset + half + j, offset + j] = -1.0
            perm[offset + j, offset + half + j] = 1.0
        offset += size
    return lanes, perm


def nt(a, b):
    return lax.dot_general(a, b, (((1,), (1,)), ((), ())), preferred_element_type=F32)


def tn(a, b):
    return lax.dot_general(a, b, (((0,), (0,)), ((), ())), preferred_element_type=F32)


def kernel(
    n, chunks,
    slab_ref, q_hbm, k_hbm, v_hbm, tk_hbm, tv_hbm, mask_ref, qg_ref, kg_ref, lanes_ref, perm_ref, w_ref,
    out_ref,
    kv, tb, qs, o_send, o_recv, o_own, lse_own, o_all, w, w_far, h_mine, h_send, h_recv, acc, tabs,
    q_ref, k_ref, v_ref, tk_ref, tv_ref,
    kv_ss, kv_rs, tb_ss, tb_rs, q_ss, q_rs, o_ss, o_rs, h_ss, h_rs, wf_ss, wf_rs, w_sem, in_sem,
):
    rows, width = q_ref.shape
    heads = width // HEAD
    trows = tk_ref.shape[0]
    keys = rows + trows
    a = n // GROUP
    g, s, t = lax.axis_index("grp"), lax.axis_index("seq"), lax.axis_index("tp")
    u, low = s // GROUP, s % GROUP
    zdev = (g, s + 2 - 4 * (low // 2), t)
    ydev = (g, s + 1 - 2 * (low % 2), t)
    tdev = (g, s, 1 - t)
    fwd = [(g, lax.rem(u + j, a) * GROUP + low, t) for j in range(a)]
    back = [(g, lax.rem(u + a - j, a) * GROUP + low, t) for j in range(a)]

    barrier = pltpu.get_barrier_semaphore()
    friends = [zdev, ydev, tdev] + fwd[1:]
    for dev in friends:
        pl.semaphore_signal(barrier, inc=1, device_id=dev, device_id_type=MESH)

    loads = [
        pltpu.make_async_copy(x, y, in_sem.at[i])
        for i, (x, y) in enumerate(
            ((k_hbm, k_ref), (tk_hbm, tk_ref), (v_hbm, v_ref), (tv_hbm, tv_ref), (q_hbm, q_ref))
        )
    ]
    for load in loads:
        load.start()
    w_copy = pltpu.make_async_copy(w_ref, w, w_sem)
    w_copy.start()

    def remote(src, dst, ss, rs, dev):
        return pltpu.make_async_remote_copy(
            src_ref=src, dst_ref=dst, send_sem=ss, recv_sem=rs, device_id=dev, device_id_type=MESH
        )

    def kv_z(h):
        return remote(kv.at[0, h], kv.at[1, h], kv_ss.at[0, h], kv_rs.at[0, h], zdev)

    def kv_y(h):
        return remote(kv.at[0, h], kv.at[2, h], kv_ss.at[1, h], kv_rs.at[1, h], ydev)

    def kv_relay(h):
        return remote(kv.at[1, h], kv.at[3, h], kv_ss.at[2, h], kv_rs.at[2, h], ydev)

    def q_move(j, h):
        return remote(qs.at[0, h], qs.at[j, h], q_ss.at[j - 1, h], q_rs.at[j - 1, h], fwd[j])

    def o_move(j, h):
        return remote(
            o_send.at[j - 1, h], o_recv.at[j - 1, h], o_ss.at[j - 1, h], o_rs.at[j - 1, h], back[j]
        )

    tb_z = remote(tb.at[0], tb.at[1], tb_ss.at[0], tb_rs.at[0], zdev)
    tb_y = remote(tb.at[0], tb.at[2], tb_ss.at[1], tb_rs.at[1], ydev)
    tb_relay = remote(tb.at[1], tb.at[3], tb_ss.at[2], tb_rs.at[2], ydev)

    freq, part, lead = lanes_ref[0:1, :], lanes_ref[1:2, :], lanes_ref[2:3, :]
    blocks = rows // WIDE
    block = lax.broadcasted_iota(jnp.int32, (blocks, HEAD), 0)
    slab = slab_ref[0] * SLAB_H
    place = jnp.where(part < 0.5, (block // SLAB_H).astype(F32), (slab + block % SLAB_H).astype(F32)) * freq
    across = lax.broadcasted_iota(jnp.int32, (WIDE, HEAD), 0).astype(F32) * freq
    trig = (jnp.cos(place), jnp.cos(across)), (jnp.sin(place), jnp.sin(across))

    def partner(x):
        wide = jnp.broadcast_to(x, (8, HEAD))
        near, far = PARTS[0] // 2, PARTS[1] // 2
        after = jnp.where(part < 0.5, pltpu.roll(wide, HEAD - near, 1), pltpu.roll(wide, HEAD - far, 1))
        before = jnp.where(part < 0.5, pltpu.roll(wide, near, 1), pltpu.roll(wide, far, 1))
        return jnp.where(lead > 0.5, after, before)[0:1]

    def h_move(h):
        return remote(h_send.at[h], h_recv.at[h], h_ss.at[h], h_rs.at[h], tdev)

    w_move = remote(w, w_far, wf_ss, wf_rs, tdev)

    scale_q = F32(1.0) / jnp.sqrt(F32(HEAD))
    kg = kg_ref[...]
    qg = qg_ref[...] * scale_q
    for which, (by_block, by_column) in enumerate(trig):
        for gain, index in ((qg, 0), (kg, 2)):
            gain = gain if which == 0 else partner(gain)
            for i in range(blocks):
                full = jnp.where(part < 1.5, by_block[i : i + 1], by_column)
                tabs[index + which, i * WIDE : (i + 1) * WIDE, :] = full * gain
    row = lax.broadcasted_iota(jnp.int32, (trows, trows), 0)
    col = lax.broadcasted_iota(jnp.int32, (trows, trows), 1)
    mark = jnp.where((row == col) & (mask_ref[...] != 1), F32(NEGATIVE), F32(0.0))
    tb[0] = jnp.broadcast_to(jnp.sum(mark, axis=1, keepdims=True), (trows, HEAD)).astype(BF16)

    def norm_scale(x32):
        return lax.rsqrt(jnp.mean(x32 * x32, axis=-1, keepdims=True) + 0.05)

    def rotated(x, which):
        x32 = x.astype(F32)
        turned = jnp.dot(x, perm_ref[...], preferred_element_type=F32)
        return ((x32 * tabs[which] + turned * tabs[which + 1]) * norm_scale(x32)).astype(BF16)

    def prepare(h):
        cols = pl.ds(pl.multiple_of(h * HEAD, HEAD), HEAD)
        kv[0, h, 0:rows, :] = rotated(k_ref[:, cols], 2)
        tk = tk_ref[:, cols].astype(F32)
        kv[0, h, rows:keys, :] = (tk * norm_scale(tk) * kg).astype(BF16)
        kv[0, h, keys : keys + rows, :] = v_ref[:, cols]
        kv[0, h, keys + rows : 2 * keys, :] = tv_ref[:, cols]
        qs[0, h] = rotated(q_ref[:, cols], 0)

    def send(h, ready):
        for lead, start in ((LEAD_Y, send_y), (LEAD_Z, send_z), (LEAD_Q, send_q)):
            if ready is None:

                @pl.when(h < lead)
                def _(start=start):
                    start(h)
            else:

                @pl.when(h + lead < heads)
                def _(start=start, lead=lead):
                    start(h + lead)

    def send_y(h):
        kv_y(h).start()

    def send_z(h):
        kv_z(h).start()

    def send_q(h):
        for j in range(1, a):
            q_move(j, h).start()

    for load in loads:
        load.wait()
    prepare(0)
    pl.semaphore_wait(barrier, len(friends))
    tb_z.start()
    tb_y.start()
    send(0, None)

    def first(h, c):
        prepare(h)
        send(h, None)
        return c

    lax.fori_loop(1, heads, first, 0)
    tb_z.wait_recv()
    tb_relay.start()
    kv_z(0).wait_recv()
    kv_relay(0).start()
    w_copy.wait()
    w_move.start()
    half = rows // 2

    def attend(j, h):
        queries = qs[j, h]
        scores = []
        top = None
        for slot in range(GROUP):
            sc = nt(kv[slot, h, 0:keys, :], queries)
            mark = tb[slot].astype(F32)
            mark = jnp.concatenate([mark] * (rows // HEAD), axis=1)
            sc = jnp.concatenate([sc[0:rows], sc[rows:keys] + mark], axis=0)
            peak = jnp.max(sc, axis=0, keepdims=True)
            top = peak if top is None else jnp.maximum(top, peak)
            scores.append(sc)
        total = None
        acc = None
        for slot in range(GROUP):
            p = jnp.exp(scores[slot] - top)
            part = jnp.sum(p, axis=0, keepdims=True)
            mixed = tn(kv[slot, h, keys : 2 * keys, :], p.astype(BF16))
            total = part if total is None else total + part
            acc = mixed if acc is None else acc + mixed
        return acc / total, top + jnp.log(total)

    def main(h, c):
        @pl.when(h + 1 < heads)
        def _():
            kv_z(h + 1).wait_recv()
            kv_relay(h + 1).start()

        send(h, True)

        kv_y(h).wait_recv()

        @pl.when(h == 0)
        def _():
            tb_y.wait_recv()
            tb_relay.wait_recv()

        for j in range(1, a):
            q_move(j, h).wait_recv()
        kv_relay(h).wait_recv()
        for j in range(1, a):
            o, lse = attend(j, h)
            high = lse.astype(BF16)
            rest = lse - high.astype(F32)
            mid = rest.astype(BF16)
            tail = (rest - mid.astype(F32)).astype(BF16)
            o_send[j - 1, h, HEAD : HEAD + 16, :] = jnp.concatenate(
                [high.astype(F32), mid.astype(F32), tail.astype(F32), jnp.zeros((13, rows), F32)], axis=0
            ).astype(BF16)
            o_send[j - 1, h, 0:HEAD, :] = o.astype(BF16)
            o_move(j, h).start()
        o, lse = attend(0, h)
        o_own[h] = o
        lse_own[h] = jnp.broadcast_to(lse, (8, rows))

        @pl.when(h > 0)
        def _():
            merge(h - 1)

        return c

    def merge(h):
        lses = [lse_own[h][0:1]]
        parts = [o_own[h]]
        for j in range(1, a):
            o_move(j, h).wait_recv()
            stats = o_recv[j - 1, h, HEAD : HEAD + 16, :].astype(F32)
            lses.append(stats[0:1] + stats[1:2] + stats[2:3])
            parts.append(o_recv[j - 1, h, 0:HEAD, :].astype(F32))
        top = functools.reduce(jnp.maximum, lses)
        shares = [jnp.exp(x - top) for x in lses]
        total = functools.reduce(jnp.add, shares)
        o = functools.reduce(jnp.add, [x * y for x, y in zip(parts, shares)]) / total
        o_all[...] = o.astype(BF16)
        h_send[h] = o_all[:, pl.ds(pl.multiple_of((1 - t) * half, half), half)].T
        h_move(h).start()
        cols = pl.ds(pl.multiple_of(h * HEAD, HEAD), HEAD)
        h_mine[:, cols] = o_all[:, pl.ds(pl.multiple_of(t * half, half), half)].T

    lax.fori_loop(0, heads, main, 0)

    step = w.shape[1] // chunks
    spans = [slice(i * step, (i + 1) * step) for i in range(chunks)]
    early = (heads - 1) * HEAD

    def dot(x, y):
        return jnp.dot(x, y, preferred_element_type=F32)

    for span in spans:
        acc[0, :, span] = dot(h_mine[:, :early], w[:early, span])
    w_move.wait_recv()
    for h in range(heads - 1):
        h_move(h).wait_recv()
    theirs = jnp.concatenate([h_recv[h] for h in range(heads - 1)], axis=1)
    for span in spans:
        acc[1, :, span] = dot(theirs, w_far[:early, span])
    merge(heads - 1)
    for span in spans:
        acc[0, :, span] += dot(h_mine[:, early:], w[early:, span])
    h_move(heads - 1).wait_recv()
    for span in spans:
        far = acc[1, :, span] + dot(h_recv[heads - 1], w_far[early:, span])
        near = acc[0, :, span]
        out_ref[:, span] = (near.astype(BF16).astype(F32) + far.astype(BF16).astype(F32)).astype(BF16)

    def drain(h, c):
        kv_z(h).wait_send()
        kv_y(h).wait_send()
        kv_relay(h).wait_send()
        h_move(h).wait_send()
        for j in range(1, a):
            q_move(j, h).wait_send()
            o_move(j, h).wait_send()
        return c

    lax.fori_loop(0, heads, drain, 0)
    tb_z.wait_send()
    tb_y.wait_send()
    tb_relay.wait_send()
    w_move.wait_send()


def body(
    n,
    visual_q, visual_key_input, visual_v, text_k, text_v, text_mask, slab_order, q_gain, key_norm_gain, w_out,
):
    rows, width = visual_q.shape
    heads = width // HEAD
    model = w_out.shape[1]
    a = n // GROUP
    trows = -(-text_k.shape[0] // 16) * 16
    pad = trows - text_k.shape[0]
    if pad:
        text_k = jnp.pad(text_k, ((0, pad), (0, 0)))
        text_v = jnp.pad(text_v, ((0, pad), (0, 0)))
        text_mask = jnp.pad(text_mask, (0, pad))
    lanes, perm = lane_constants()
    chunks = 6 if model % (6 * HEAD) == 0 else 1
    keys = rows + trows
    half = rows // 2
    peers = a - 1
    vm = pl.BlockSpec(memory_space=pltpu.VMEM)
    anywhere = pl.BlockSpec(memory_space=pl.ANY)
    dma = pltpu.SemaphoreType.DMA
    return pl.pallas_call(
        functools.partial(kernel, n, chunks),
        out_shape=pltpu.VMEM((half, model), BF16),
        in_specs=[pl.BlockSpec(memory_space=pltpu.SMEM)] + [anywhere] * 5 + [vm] * 5 + [anywhere],
        out_specs=vm,
        scratch_shapes=[
            pltpu.VMEM((GROUP, heads, 2 * keys, HEAD), BF16),
            pltpu.VMEM((GROUP, trows, HEAD), BF16),
            pltpu.VMEM((a, heads, rows, HEAD), BF16),
            pltpu.VMEM((peers, heads, HEAD + 16, rows), BF16),
            pltpu.VMEM((peers, heads, HEAD + 16, rows), BF16),
            pltpu.VMEM((heads, HEAD, rows), F32),
            pltpu.VMEM((heads, 8, rows), F32),
            pltpu.VMEM((HEAD, rows), BF16),
            pltpu.VMEM(w_out.shape, BF16),
            pltpu.VMEM(w_out.shape, BF16),
            pltpu.VMEM((half, width), BF16),
            pltpu.VMEM((heads, half, HEAD), BF16),
            pltpu.VMEM((heads, half, HEAD), BF16),
            pltpu.VMEM((2, half, model), F32),
            pltpu.VMEM((4, rows, HEAD), F32),
            *[pltpu.VMEM(x.shape, BF16) for x in (visual_q, visual_key_input, visual_v, text_k, text_v)],
            dma((3, heads)), dma((3, heads)), dma((3,)), dma((3,)),
            dma((peers, heads)), dma((peers, heads)), dma((peers, heads)), dma((peers, heads)),
            dma((heads,)), dma((heads,)), dma, dma, dma, dma((5,)),
        ],
        compiler_params=pltpu.CompilerParams(
            collective_id=0, has_side_effects=True, vmem_limit_bytes=60 * 1024 * 1024
        ),
    )(
        slab_order, visual_q, visual_key_input, visual_v, text_k, text_v, text_mask[None], q_gain[None],
        key_norm_gain[None], jnp.asarray(lanes), jnp.asarray(perm, BF16), w_out,
    )


def solution(mesh):
    rows = P(("grp", "seq"), "tp")
    placed = (rows,) * 5 + (P(("grp", "seq")),) * 2 + (P(), P(), P("tp", None))
    return jax.shard_map(
        functools.partial(body, mesh.shape["seq"]),
        mesh=mesh, in_specs=placed, out_specs=P(("grp", "seq", "tp"), None), check_vma=False,
    )
```

profile of v0, /device:TPU:1, one launch (start us, length us, event | category | flops | bytes accessed | tf_op | source)
XLA Modules:
  0.0 54.0 jit_solution(14671980984702911173)
XLA Ops:
  0.7 52.4 %shard_map.118 = bf16[128,3072]{1,0:T(8,128)(2,1)S(1)} custom-call(s32[1]{0:T(128)S(6)} %copy.15.slab_ref, bf16[256,768]{1,0:T(8,128)(2,1)} %q_hbm.1, bf16[256,768]{1,0:T(8,128)(2,1)} %k_hbm.1, bf16[256,768]{1,0:T(8,128)(2,1)} %v_hbm.1, bf16[32,768]{1,0:T(8,128)(2,1)} %tk_hbm.1, bf16[32,768]{1,0:T(8,128)(2,1)} %tv_hbm.1, s32[1,32]{1,0:T(1,128)} %bitcast.3, ...), custom_call_target="tpu_custom_call" | custom-call | tf_op jit(solution)/shard_map/pallas_call | solution.py:352
  53.1 0.9 %copy.14 = bf16[128,3072]{1,0:T(8,128)(2,1)} copy(bf16[128,3072]{1,0:T(8,128)(2,1)S(1)} %shard_map.118) | data formatting | bytes 1572864
where the time goes:
time: 54.6 us; the launch traced here: 54 us
  Pallas kernels  52.4 us (96%)
  local copies, waits for them, and re-layouts  0.88 us (2%)
  between operations  0.66 us (1%)
    pallas_call x1, Pallas kernels, body(): pl.pallas_call(functools.partial(kernel, n, chunks), out_shape=pltpu.VMEM...  52.4 us

commit v1 on v0

--- a/solution.py
+++ b/solution.py
@@ -18,6 +18,8 @@
 BF16 = jnp.bfloat16
 LEAD_Y, LEAD_Z, LEAD_Q = 2, 2, 2
 GROUP = 4
+STATS = 16
+HUB_SLOTS = 8
 
 
 def lane_constants():
@@ -325,6 +327,456 @@
     tb_y.wait_send()
     tb_relay.wait_send()
     w_move.wait_send()
+
+
+def hub_kernel(
+    chunks,
+    slab_ref, q_hbm, k_hbm, v_hbm, tk_hbm, tv_hbm, mask_ref, qg_ref, kg_ref, lanes_ref, perm_ref, w_ref,
+    out_ref,
+    mine, held, tb, q_mine, q_held, o_send, o_recv, scores_a, scores_b, o_all, w, w_far, h_mine, h_send, h_recv,
+    acc, tabs, q_ref, k_ref, v_ref, tk_ref, tv_ref,
+    kv_ss, kv_rs, tb_ss, tb_rs, q_ss, q_rs, o_ss, o_rs, h_ss, h_rs, wf_ss, wf_rs, w_sem, in_sem,
+):
+    rows, width = q_ref.shape
+    heads = width // HEAD
+    trows = tk_ref.shape[0]
+    keys = rows + trows
+    half = rows // 2
+    pairs = heads // 2
+    g, s, t = lax.axis_index("grp"), lax.axis_index("seq"), lax.axis_index("tp")
+    u, low = s // GROUP, s % GROUP
+    row, col = low // 2, low % 2
+    inner = row + u == 1
+    outer = row + u != 1
+    aside = 1 - 2 * col
+
+    def dev(seq):
+        return (g, seq, t)
+
+    near_s, far_s, cross_s = s + 2 - 4 * row, s + 2 - 4 * u, s + GROUP - 2 * GROUP * u
+    near, far, cross, ydev = dev(near_s), dev(far_s), dev(cross_s), dev(s + aside)
+    near_y, far_y, cross_y = dev(near_s + aside), dev(far_s + aside), dev(cross_s + aside)
+    tdev = (g, s, 1 - t)
+
+    barrier = pltpu.get_barrier_semaphore()
+    friends = [near, ydev, tdev]
+    for friend in friends:
+        pl.semaphore_signal(barrier, inc=1, device_id=friend, device_id_type=MESH)
+
+    @pl.when(inner)
+    def _():
+        pl.semaphore_signal(barrier, inc=1, device_id=far, device_id_type=MESH)
+
+    loads = [
+        pltpu.make_async_copy(x, y, in_sem.at[i])
+        for i, (x, y) in enumerate(
+            ((q_hbm, q_ref), (k_hbm, k_ref), (tk_hbm, tk_ref), (v_hbm, v_ref), (tv_hbm, tv_ref))
+        )
+    ]
+    for load in loads:
+        load.start()
+    w_copy = pltpu.make_async_copy(w_ref, w, w_sem)
+    w_copy.start()
+
+    def remote(src, dst, ss, rs, to):
+        return pltpu.make_async_remote_copy(
+            src_ref=src, dst_ref=dst, send_sem=ss, recv_sem=rs, device_id=to, device_id_type=MESH
+        )
+
+    def mine_on(i):
+        return 2 * i + col
+
+    def mine_off(i):
+        return 2 * i + 1 - col
+
+    def kv_move(src, slot, kind, i, to):
+        return remote(src, held.at[slot - 1, i], kv_ss.at[kind, i], kv_rs.at[slot - 1, i], to)
+
+    def kv_in(i):
+        return kv_move(mine.at[mine_on(i)], 1, 0, i, near)
+
+    def kv_off(i):
+        return kv_move(mine.at[mine_off(i)], 2, 1, i, ydev)
+
+    def kv_relay(i):
+        return kv_move(held.at[1, i], 3, 2, i, near)
+
+    def q_move(src, slot, kind, i, to):
+        return remote(src, q_held.at[slot - 1, i], q_ss.at[kind, i], q_rs.at[slot - 1, i], to)
+
+    def q_in(i):
+        return q_move(q_mine.at[mine_on(i)], 1, 0, i, near)
+
+    def q_off(i):
+        return q_move(q_mine.at[mine_off(i)], 4, 1, i, ydev)
+
+    def q_relay(i):
+        return q_move(q_held.at[3, i], 5, 2, i, near)
+
+    def q_far(slot, i):
+        if slot == 2:
+            return q_move(q_mine.at[mine_on(i)], 2, 0, i, far)
+        kind, start = {3: (2, 1), 6: (3, 4), 7: (4, 5)}[slot]
+        return q_move(q_held.at[start - 1, i], slot, kind, i, far)
+
+    def o_move(slot, i):
+        index, to = {
+            1: (0, near), 4: (0, ydev), 5: (0, near_y),
+            2: (1, far), 3: (1, cross), 6: (1, far_y), 7: (1, cross_y),
+        }[slot]
+        h = mine_on(i)
+        return remote(
+            o_send.at[slot - 1, i], o_recv.at[index, h], o_ss.at[slot - 1, i], o_rs.at[index, h], to
+        )
+
+    def h_move(h):
+        return remote(h_send.at[h], h_recv.at[h], h_ss.at[h], h_rs.at[h], tdev)
+
+    w_move = remote(w, w_far, wf_ss, wf_rs, tdev)
+    tb_in = remote(tb.at[0], tb.at[1], tb_ss.at[0], tb_rs.at[0], near)
+    tb_y = remote(tb.at[0], tb.at[2], tb_ss.at[1], tb_rs.at[1], ydev)
+    tb_relay = remote(tb.at[2], tb.at[3], tb_ss.at[2], tb_rs.at[2], near)
+
+    freq, part, lead = lanes_ref[0:1, :], lanes_ref[1:2, :], lanes_ref[2:3, :]
+    blocks = rows // WIDE
+    block = lax.broadcasted_iota(jnp.int32, (blocks, HEAD), 0)
+    slab = slab_ref[0] * SLAB_H
+    place = jnp.where(part < 0.5, (block // SLAB_H).astype(F32), (slab + block % SLAB_H).astype(F32)) * freq
+    across = lax.broadcasted_iota(jnp.int32, (WIDE, HEAD), 0).astype(F32) * freq
+    trig = (jnp.cos(place), jnp.cos(across)), (jnp.sin(place), jnp.sin(across))
+
+    def partner(x):
+        wide = jnp.broadcast_to(x, (8, HEAD))
+        near, far = PARTS[0] // 2, PARTS[1] // 2
+        after = jnp.where(part < 0.5, pltpu.roll(wide, HEAD - near, 1), pltpu.roll(wide, HEAD - far, 1))
+        before = jnp.where(part < 0.5, pltpu.roll(wide, near, 1), pltpu.roll(wide, far, 1))
+        return jnp.where(lead > 0.5, after, before)[0:1]
+
+    scale_q = F32(1.0) / jnp.sqrt(F32(HEAD))
+    kg = kg_ref[...]
+    qg = qg_ref[...] * scale_q
+    for which, (by_block, by_column) in enumerate(trig):
+        for gain, index in ((qg, 0), (kg, 2)):
+            gain = gain if which == 0 else partner(gain)
+            for i in range(blocks):
+                full = jnp.where(part < 1.5, by_block[i : i + 1], by_column)
+                tabs[index + which, i * WIDE : (i + 1) * WIDE, :] = full * gain
+    line = lax.broadcasted_iota(jnp.int32, (trows, trows), 0)
+    lane = lax.broadcasted_iota(jnp.int32, (trows, trows), 1)
+    mark = jnp.where((line == lane) & (mask_ref[...] != 1), F32(NEGATIVE), F32(0.0))
+    tb[0] = jnp.broadcast_to(jnp.sum(mark, axis=1, keepdims=True), (trows, HEAD)).astype(BF16)
+
+    def norm_scale(x32):
+        return lax.rsqrt(jnp.mean(x32 * x32, axis=-1, keepdims=True) + 0.05)
+
+    def rotated(x, which):
+        x32 = x.astype(F32)
+        turned = jnp.dot(x, perm_ref[...], preferred_element_type=F32)
+        return ((x32 * tabs[which] + turned * tabs[which + 1]) * norm_scale(x32)).astype(BF16)
+
+    def prepare_q(h):
+        q_mine[h] = rotated(q_ref[:, pl.ds(pl.multiple_of(h * HEAD, HEAD), HEAD)], 0)
+
+    def prepare_kv(h):
+        cols = pl.ds(pl.multiple_of(h * HEAD, HEAD), HEAD)
+        mine[h, 0:rows, :] = rotated(k_ref[:, cols], 2)
+        tk = tk_ref[:, cols].astype(F32)
+        mine[h, rows:keys, :] = (tk * norm_scale(tk) * kg).astype(BF16)
+        mine[h, keys : keys + rows, :] = v_ref[:, cols]
+        mine[h, keys + rows : 2 * keys, :] = tv_ref[:, cols]
+
+    def side(slot, i, part):
+        where = pl.ds(part * keys, keys)
+        return held[slot - 1, i, where, :] if slot else mine[mine_on(i), where, :]
+
+    def score(slot, i, where):
+        queries = q_held[slot - 1, i] if slot else q_mine[mine_on(i)]
+        top = None
+        for n in range(GROUP):
+            sc = nt(side(n, i, 0), queries)
+            mark = tb[n].astype(F32)
+            mark = jnp.concatenate([mark] * (rows // HEAD), axis=1)
+            sc = jnp.concatenate([sc[0:rows], sc[rows:keys] + mark], axis=0)
+            where[n] = sc
+            peak = jnp.max(sc, axis=0, keepdims=True)
+            top = peak if top is None else jnp.maximum(top, peak)
+        return top
+
+    def weigh(i, where, top):
+        total = None
+        mixed = None
+        for n in range(GROUP):
+            p = jnp.exp(where[n] - top)
+            amount = jnp.sum(p, axis=0, keepdims=True)
+            got = tn(side(n, i, 1), p.astype(BF16))
+            total = amount if total is None else total + amount
+            mixed = got if mixed is None else mixed + got
+        return mixed / total, top + jnp.log(total)
+
+    wides = rows // HEAD
+
+    def pack(to, o, lse):
+        high = lse.astype(BF16).astype(F32)
+        rest = lse - high
+        mid = rest.astype(BF16).astype(F32)
+        pieces = [x[:, i * HEAD : (i + 1) * HEAD] for x in (high, mid, rest - mid) for i in range(wides)]
+        pieces.append(jnp.zeros((STATS - 3 * wides, HEAD), F32))
+        to[rows : rows + STATS, :] = jnp.concatenate(pieces, axis=0).astype(BF16)
+        for i in range(wides):
+            to[i * HEAD : (i + 1) * HEAD, :] = o[:, i * HEAD : (i + 1) * HEAD].astype(BF16)
+
+    def unpack(index, h):
+        o = jnp.concatenate([o_recv[index, h, i * HEAD : (i + 1) * HEAD, :] for i in range(wides)], axis=1)
+        stats = o_recv[index, h, rows : rows + STATS, :].astype(F32)
+        levels = [
+            jnp.concatenate([stats[k * wides + i : k * wides + i + 1] for i in range(wides)], axis=1)
+            for k in range(3)
+        ]
+        return o.astype(F32), levels[0] + levels[1] + levels[2]
+
+    def merge(h):
+        @pl.when(jnp.logical_or(outer, h % 2 != col))
+        def _():
+            remote(
+                o_send.at[0, 0], o_recv.at[0, h], o_ss.at[0, 0], o_rs.at[0, h], near
+            ).wait_recv()
+
+        remote(o_send.at[0, 0], o_recv.at[1, h], o_ss.at[0, 0], o_rs.at[1, h], near).wait_recv()
+        (o, lse), (o_, lse_) = unpack(0, h), unpack(1, h)
+        share = 1.0 / (1.0 + jnp.exp(lse_ - lse))
+        o_all[...] = (o * share + o_ * (1.0 - share)).astype(BF16)
+        h_send[h] = o_all[:, pl.ds(pl.multiple_of((1 - t) * half, half), half)].T
+        h_move(h).start()
+        cols = pl.ds(pl.multiple_of(h * HEAD, HEAD), HEAD)
+        h_mine[:, cols] = o_all[:, pl.ds(pl.multiple_of(t * half, half), half)].T
+
+    loads[0].wait()
+    prepare_q(mine_off(0))
+    prepare_q(mine_on(0))
+
+    @pl.when(inner)
+    def _():
+        pl.semaphore_wait(barrier, len(friends) + 1)
+        q_far(2, 0).start()
+
+    @pl.when(outer)
+    def _():
+        pl.semaphore_wait(barrier, len(friends))
+        q_in(0).start()
+        tb_in.start()
+
+    q_off(0).start()
+    tb_y.start()
+    for load in loads[1:]:
+        load.wait()
+    prepare_kv(mine_on(0))
+
+    @pl.when(outer)
+    def _():
+        kv_in(0).start()
+
+    def queries(i, c):
+        prepare_q(mine_off(i))
+        q_off(i).start()
+        prepare_q(mine_on(i))
+
+        @pl.when(inner)
+        def _():
+            q_far(2, i).start()
+
+        @pl.when(outer)
+        def _():
+            q_in(i).start()
+
+        return c
+
+    lax.fori_loop(1, pairs, queries, 0)
+    prepare_kv(mine_off(0))
+    kv_off(0).start()
+
+    def keep(i, c):
+        prepare_kv(mine_off(i))
+        kv_off(i).start()
+        prepare_kv(mine_on(i))
+        return c
+
+    lax.fori_loop(1, pairs, keep, 0)
+
+    @pl.when(outer)
+    def _():
+        tb_y.wait_recv()
+        tb_relay.start()
+
+        def pass_queries(i, c):
+            q_off(i).wait_recv()
+            q_relay(i).start()
+            return c
+
+        lax.fori_loop(0, pairs, pass_queries, 0)
+
+        def pass_keys(i, c):
+            @pl.when(i > 0)
+            def _():
+                kv_in(i).start()
+
+            kv_off(i).wait_recv()
+            kv_relay(i).start()
+            return c
+
+        lax.fori_loop(0, pairs, pass_keys, 0)
+
+    w_copy.wait()
+    w_move.start()
+
+    @pl.when(outer)
+    def _():
+        def collect(h, c):
+            merge(h)
+            return c
+
+        lax.fori_loop(0, heads - 2, collect, 0)
+
+    @pl.when(inner)
+    def _():
+        def onward(i, c):
+            q_in(i).wait_recv()
+            q_far(3, i).start()
+            q_off(i).wait_recv()
+            q_far(6, i).start()
+            return c
+
+        def onward_last(i, c):
+            q_relay(i).wait_recv()
+            q_far(7, i).start()
+            return c
+
+        lax.fori_loop(0, pairs, onward, 0)
+        lax.fori_loop(0, pairs, onward_last, 0)
+        tb_in.wait_recv()
+        tb_y.wait_recv()
+        tb_relay.wait_recv()
+
+        def main(i, c):
+            kv_in(i).wait_recv()
+            kv_off(i).wait_recv()
+
+            for slot in (2, 3, 6, 7):
+                q_far(slot, i).wait_recv()
+            kv_relay(i).wait_recv()
+            order = (7, 3, 6, 2, 5, 1, 4, 0)
+            top = score(order[0], i, scores_a)
+            for n, slot in enumerate(order):
+                here, there = ((scores_a, scores_b), (scores_b, scores_a))[n % 2]
+                after = score(order[n + 1], i, there) if n + 1 < HUB_SLOTS else None
+                o, lse = weigh(i, here, top)
+                top = after
+                if slot:
+                    pack(o_send.at[slot - 1, i], o, lse)
+                    o_move(slot, i).start()
+                else:
+                    pack(o_recv.at[0, mine_on(i)], o, lse)
+
+            @pl.when(i > 0)
+            def _():
+                merge(2 * i - 2)
+                merge(2 * i - 1)
+
+            return c
+
+        lax.fori_loop(0, pairs, main, 0)
+
+    step = w.shape[1] // chunks
+    spans = [slice(i * step, (i + 1) * step) for i in range(chunks)]
+    early = (heads - 2) * HEAD
+
+    def dot(x, y):
+        return jnp.dot(x, y, preferred_element_type=F32)
+
+    for span in spans:
+        acc[0, :, span] = dot(h_mine[:, :early], w[:early, span])
+    w_move.wait_recv()
+    for h in range(heads - 2):
+        h_move(h).wait_recv()
+    theirs = jnp.concatenate([h_recv[h] for h in range(heads - 2)], axis=1)
+    for span in spans:
+        acc[1, :, span] = dot(theirs, w_far[:early, span])
+
+    merge(heads - 2)
+    merge(heads - 1)
+
+    for span in spans:
+        acc[0, :, span] += dot(h_mine[:, early:], w[early:, span])
+    h_move(heads - 2).wait_recv()
+    h_move(heads - 1).wait_recv()
+    last = jnp.concatenate([h_recv[heads - 2], h_recv[heads - 1]], axis=1)
+    for span in spans:
+        theirs = acc[1, :, span] + dot(last, w_far[early:, span])
+        mine_too = acc[0, :, span]
+        out_ref[:, span] = (mine_too.astype(BF16).astype(F32) + theirs.astype(BF16).astype(F32)).astype(BF16)
+
+    def drain(i, c):
+        q_off(i).wait_send()
+        kv_off(i).wait_send()
+
+        @pl.when(inner)
+        def _():
+            for slot in (2, 3, 6, 7):
+                q_far(slot, i).wait_send()
+            for slot in range(1, HUB_SLOTS):
+                o_move(slot, i).wait_send()
+
+        @pl.when(outer)
+        def _():
+            q_in(i).wait_send()
+            kv_in(i).wait_send()
+            q_relay(i).wait_send()
+            kv_relay(i).wait_send()
+
+        return c
+
+    lax.fori_loop(0, pairs, drain, 0)
+
+    tb_y.wait_send()
+
+    @pl.when(outer)
+    def _():
+        tb_in.wait_send()
+        tb_relay.wait_send()
+
+    def settle(h, c):
+        h_move(h).wait_send()
+        return c
+
+    lax.fori_loop(0, heads, settle, 0)
+    w_move.wait_send()
+
+
+def hub_scratch(rows, trows, heads, model, w_shape, inputs):
+    keys, half, pairs = rows + trows, rows // 2, heads // 2
+    dma = pltpu.SemaphoreType.DMA
+    return [
+        pltpu.VMEM((heads, 2 * keys, HEAD), BF16),
+        pltpu.VMEM((3, pairs, 2 * keys, HEAD), BF16),
+        pltpu.VMEM((GROUP, trows, HEAD), BF16),
+        pltpu.VMEM((heads, rows, HEAD), BF16),
+        pltpu.VMEM((HUB_SLOTS - 1, pairs, rows, HEAD), BF16),
+        pltpu.VMEM((HUB_SLOTS - 1, pairs, rows + STATS, HEAD), BF16),
+        pltpu.VMEM((2, heads, rows + STATS, HEAD), BF16),
+        pltpu.VMEM((GROUP, keys, rows), F32),
+        pltpu.VMEM((GROUP, keys, rows), F32),
+        pltpu.VMEM((HEAD, rows), BF16),
+        pltpu.VMEM(w_shape, BF16),
+        pltpu.VMEM(w_shape, BF16),
+        pltpu.VMEM((half, heads * HEAD), BF16),
+        pltpu.VMEM((heads, half, HEAD), BF16),
+        pltpu.VMEM((heads, half, HEAD), BF16),
+        pltpu.VMEM((2, half, model), F32),
+        pltpu.VMEM((4, rows, HEAD), F32),
+        *[pltpu.VMEM(x.shape, BF16) for x in inputs],
+        dma((3, pairs)), dma((3, pairs)), dma((3,)), dma((3,)),
+        dma((5, pairs)), dma((HUB_SLOTS - 1, pairs)), dma((HUB_SLOTS - 1, pairs)), dma((2, heads)),
+        dma((heads,)), dma((heads,)), dma, dma, dma, dma((5,)),
+    ]
 
 
 def body(
@@ -349,39 +801,46 @@
     vm = pl.BlockSpec(memory_space=pltpu.VMEM)
     anywhere = pl.BlockSpec(memory_space=pl.ANY)
     dma = pltpu.SemaphoreType.DMA
+    operands = (
+        slab_order, visual_q, visual_key_input, visual_v, text_k, text_v, text_mask[None], q_gain[None],
+        key_norm_gain[None], jnp.asarray(lanes), jnp.asarray(perm, BF16), w_out,
+    )
+    if n == 2 * GROUP and rows % HEAD == 0 and heads % 2 == 0:
+        run = functools.partial(hub_kernel, chunks)
+        scratch = hub_scratch(rows, trows, heads, model, w_out.shape, operands[1:6])
+    else:
+        run = functools.partial(kernel, n, chunks)
+        scratch = [
+                pltpu.VMEM((GROUP, heads, 2 * keys, HEAD), BF16),
+                pltpu.VMEM((GROUP, trows, HEAD), BF16),
+                pltpu.VMEM((a, heads, rows, HEAD), BF16),
+                pltpu.VMEM((peers, heads, HEAD + 16, rows), BF16),
+                pltpu.VMEM((peers, heads, HEAD + 16, rows), BF16),
+                pltpu.VMEM((heads, HEAD, rows), F32),
+                pltpu.VMEM((heads, 8, rows), F32),
+                pltpu.VMEM((HEAD, rows), BF16),
+                pltpu.VMEM(w_out.shape, BF16),
+                pltpu.VMEM(w_out.shape, BF16),
+                pltpu.VMEM((half, width), BF16),
+                pltpu.VMEM((heads, half, HEAD), BF16),
+                pltpu.VMEM((heads, half, HEAD), BF16),
+                pltpu.VMEM((2, half, model), F32),
+                pltpu.VMEM((4, rows, HEAD), F32),
+                *[pltpu.VMEM(x.shape, BF16) for x in (visual_q, visual_key_input, visual_v, text_k, text_v)],
+                dma((3, heads)), dma((3, heads)), dma((3,)), dma((3,)),
+                dma((peers, heads)), dma((peers, heads)), dma((peers, heads)), dma((peers, heads)),
+                dma((heads,)), dma((heads,)), dma, dma, dma, dma((5,)),
+        ]
     return pl.pallas_call(
-        functools.partial(kernel, n, chunks),
+        run,
         out_shape=pltpu.VMEM((half, model), BF16),
         in_specs=[pl.BlockSpec(memory_space=pltpu.SMEM)] + [anywhere] * 5 + [vm] * 5 + [anywhere],
         out_specs=vm,
-        scratch_shapes=[
-            pltpu.VMEM((GROUP, heads, 2 * keys, HEAD), BF16),
-            pltpu.VMEM((GROUP, trows, HEAD), BF16),
-            pltpu.VMEM((a, heads, rows, HEAD), BF16),
-            pltpu.VMEM((peers, heads, HEAD + 16, rows), BF16),
-            pltpu.VMEM((peers, heads, HEAD + 16, rows), BF16),
-            pltpu.VMEM((heads, HEAD, rows), F32),
-            pltpu.VMEM((heads, 8, rows), F32),
-            pltpu.VMEM((HEAD, rows), BF16),
-            pltpu.VMEM(w_out.shape, BF16),
-            pltpu.VMEM(w_out.shape, BF16),
-            pltpu.VMEM((half, width), BF16),
-            pltpu.VMEM((heads, half, HEAD), BF16),
-            pltpu.VMEM((heads, half, HEAD), BF16),
-            pltpu.VMEM((2, half, model), F32),
-            pltpu.VMEM((4, rows, HEAD), F32),
-            *[pltpu.VMEM(x.shape, BF16) for x in (visual_q, visual_key_input, visual_v, text_k, text_v)],
-            dma((3, heads)), dma((3, heads)), dma((3,)), dma((3,)),
-            dma((peers, heads)), dma((peers, heads)), dma((peers, heads)), dma((peers, heads)),
-            dma((heads,)), dma((heads,)), dma, dma, dma, dma((5,)),
-        ],
+        scratch_shapes=scratch,
         compiler_params=pltpu.CompilerParams(
             collective_id=0, has_side_effects=True, vmem_limit_bytes=60 * 1024 * 1024
         ),
-    )(
-        slab_order, visual_q, visual_key_input, visual_v, text_k, text_v, text_mask[None], q_gain[None],
-        key_norm_gain[None], jnp.asarray(lanes), jnp.asarray(perm, BF16), w_out,
-    )
+    )(*operands)
 
 
 def solution(mesh):

time: 54.6 us -> 47.3 us (0.87)
  Pallas kernels: 52.4 us -> 45.6 us
    pallas_call x1, Pallas kernels: 52.4 us -> 45.6 us  [body(): pl.pallas_call(run, out_shape=pltpu.VMEM((half, model), BF16), in_specs=[...]
where the time goes in v1:
time: 47.3 us; the launch traced here: 47.1 us
  Pallas kernels  45.6 us (96%)
  local copies, waits for them, and re-layouts  0.88 us (2%)
  between operations  0.66 us (1%)
    pallas_call x1, Pallas kernels, body(): pl.pallas_call(run, out_shape=pltpu.VMEM((half, model), BF16), in_specs=[...  45.6 us

profile of v1, /device:TPU:1, one launch (start us, length us, event | category | flops | bytes accessed | tf_op | source)
XLA Modules:
  0.0 47.1 jit_solution(1537277295887270657)
XLA Ops:
  0.7 45.6 %shard_map.118 = bf16[128,3072]{1,0:T(8,128)(2,1)S(1)} custom-call(s32[1]{0:T(128)S(6)} %copy.15.slab_ref, bf16[256,768]{1,0:T(8,128)(2,1)} %q_hbm.1, bf16[256,768]{1,0:T(8,128)(2,1)} %k_hbm.1, bf16[256,768]{1,0:T(8,128)(2,1)} %v_hbm.1, bf16[32,768]{1,0:T(8,128)(2,1)} %tk_hbm.1, bf16[32,768]{1,0:T(8,128)(2,1)} %tv_hbm.1, s32[1,32]{1,0:T(1,128)} %bitcast.3, ...), custom_call_target="tpu_custom_call" | custom-call | tf_op jit(solution)/shard_map/pallas_call | solution.py:834
  46.2 0.9 %copy.14 = bf16[128,3072]{1,0:T(8,128)(2,1)} copy(bf16[128,3072]{1,0:T(8,128)(2,1)S(1)} %shard_map.118) | data formatting | bytes 1572864

commit v2 on v1

--- a/solution.py
+++ b/solution.py
@@ -18,7 +18,7 @@
 BF16 = jnp.bfloat16
 LEAD_Y, LEAD_Z, LEAD_Q = 2, 2, 2
 GROUP = 4
-STATS = 16
+STATS = 8
 HUB_SLOTS = 8
 
 
@@ -331,10 +331,10 @@
 
 def hub_kernel(
     chunks,
-    slab_ref, q_hbm, k_hbm, v_hbm, tk_hbm, tv_hbm, mask_ref, qg_ref, kg_ref, lanes_ref, perm_ref, w_ref,
+    slab_hbm, q_hbm, k_hbm, v_hbm, tk_hbm, tv_hbm, mask_hbm, qg_hbm, kg_hbm, lanes_hbm, perm_hbm, w_ref,
     out_ref,
     mine, held, tb, q_mine, q_held, o_send, o_recv, scores_a, scores_b, o_all, w, w_far, h_mine, h_send, h_recv,
-    acc, tabs, q_ref, k_ref, v_ref, tk_ref, tv_ref,
+    acc, tabs, q_ref, k_ref, v_ref, tk_ref, tv_ref, slab_ref, mask_ref, qg_ref, kg_ref, lanes_ref, perm_ref,
     kv_ss, kv_rs, tb_ss, tb_rs, q_ss, q_rs, o_ss, o_rs, h_ss, h_rs, wf_ss, wf_rs, w_sem, in_sem,
 ):
     rows, width = q_ref.shape
@@ -370,7 +370,11 @@
     loads = [
         pltpu.make_async_copy(x, y, in_sem.at[i])
         for i, (x, y) in enumerate(
-            ((q_hbm, q_ref), (k_hbm, k_ref), (tk_hbm, tk_ref), (v_hbm, v_ref), (tv_hbm, tv_ref))
+            (
+                (q_hbm, q_ref), (lanes_hbm, lanes_ref), (slab_hbm, slab_ref), (qg_hbm, qg_ref), (kg_hbm, kg_ref),
+                (perm_hbm, perm_ref), (mask_hbm, mask_ref),
+                (k_hbm, k_ref), (tk_hbm, tk_ref), (v_hbm, v_ref), (tv_hbm, tv_ref),
+            )
         )
     ]
     for load in loads:
@@ -389,35 +393,35 @@
     def mine_off(i):
         return 2 * i + 1 - col
 
-    def kv_move(src, slot, kind, i, to):
-        return remote(src, held.at[slot - 1, i], kv_ss.at[kind, i], kv_rs.at[slot - 1, i], to)
+    def kv_move(src, slot, i, to):
+        return remote(src, held.at[slot - 1, i], kv_ss, kv_rs.at[i], to)
 
     def kv_in(i):
-        return kv_move(mine.at[mine_on(i)], 1, 0, i, near)
+        return kv_move(mine.at[mine_on(i)], 1, i, near)
 
     def kv_off(i):
-        return kv_move(mine.at[mine_off(i)], 2, 1, i, ydev)
+        return kv_move(mine.at[mine_off(i)], 2, i, ydev)
 
     def kv_relay(i):
-        return kv_move(held.at[1, i], 3, 2, i, near)
-
-    def q_move(src, slot, kind, i, to):
-        return remote(src, q_held.at[slot - 1, i], q_ss.at[kind, i], q_rs.at[slot - 1, i], to)
+        return kv_move(held.at[1, i], 3, i, near)
+
+    def q_move(src, slot, i, to):
+        return remote(src, q_held.at[slot - 1, i], q_ss, q_rs.at[{1: 0, 4: 1, 5: 2}.get(slot, 3), i], to)
 
     def q_in(i):
-        return q_move(q_mine.at[mine_on(i)], 1, 0, i, near)
+        return q_move(q_mine.at[mine_on(i)], 1, i, near)
 
     def q_off(i):
-        return q_move(q_mine.at[mine_off(i)], 4, 1, i, ydev)
+        return q_move(q_mine.at[mine_off(i)], 4, i, ydev)
 
     def q_relay(i):
-        return q_move(q_held.at[3, i], 5, 2, i, near)
+        return q_move(q_held.at[3, i], 5, i, near)
 
     def q_far(slot, i):
         if slot == 2:
-            return q_move(q_mine.at[mine_on(i)], 2, 0, i, far)
-        kind, start = {3: (2, 1), 6: (3, 4), 7: (4, 5)}[slot]
-        return q_move(q_held.at[start - 1, i], slot, kind, i, far)
+            return q_move(q_mine.at[mine_on(i)], 2, i, far)
+        start = {3: 1, 6: 4, 7: 5}[slot]
+        return q_move(q_held.at[start - 1, i], slot, i, far)
 
     def o_move(slot, i):
         index, to = {
@@ -426,21 +430,29 @@
         }[slot]
         h = mine_on(i)
         return remote(
-            o_send.at[slot - 1, i], o_recv.at[index, h], o_ss.at[slot - 1, i], o_rs.at[index, h], to
+            o_send.at[slot - 1, i], o_recv.at[index, h], o_ss, o_rs.at[h], to
         )
 
     def h_move(h):
-        return remote(h_send.at[h], h_recv.at[h], h_ss.at[h], h_rs.at[h], tdev)
+        return remote(h_send.at[h], h_recv.at[h], h_ss, h_rs.at[h // (heads - 2)], tdev)
+
+    def arrived(ref, sem):
+        remote(ref, ref, sem, sem, near).wait_recv()
+
+    def left(ref, sem):
+        remote(ref, ref, sem, sem, near).wait_send()
 
     w_move = remote(w, w_far, wf_ss, wf_rs, tdev)
-    tb_in = remote(tb.at[0], tb.at[1], tb_ss.at[0], tb_rs.at[0], near)
-    tb_y = remote(tb.at[0], tb.at[2], tb_ss.at[1], tb_rs.at[1], ydev)
-    tb_relay = remote(tb.at[2], tb.at[3], tb_ss.at[2], tb_rs.at[2], near)
-
+    tb_in = remote(tb.at[0], tb.at[1], tb_ss, tb_rs, near)
+    tb_y = remote(tb.at[0], tb.at[2], tb_ss, tb_rs, ydev)
+    tb_relay = remote(tb.at[2], tb.at[3], tb_ss, tb_rs, near)
+
+    for load in loads[1:7]:
+        load.wait()
     freq, part, lead = lanes_ref[0:1, :], lanes_ref[1:2, :], lanes_ref[2:3, :]
     blocks = rows // WIDE
     block = lax.broadcasted_iota(jnp.int32, (blocks, HEAD), 0)
-    slab = slab_ref[0] * SLAB_H
+    slab = slab_ref[...] * SLAB_H
     place = jnp.where(part < 0.5, (block // SLAB_H).astype(F32), (slab + block % SLAB_H).astype(F32)) * freq
     across = lax.broadcasted_iota(jnp.int32, (WIDE, HEAD), 0).astype(F32) * freq
     trig = (jnp.cos(place), jnp.cos(across)), (jnp.sin(place), jnp.sin(across))
@@ -535,13 +547,16 @@
         return o.astype(F32), levels[0] + levels[1] + levels[2]
 
     def merge(h):
-        @pl.when(jnp.logical_or(outer, h % 2 != col))
+        hub = jnp.logical_and(inner, h % 2 == col)
+
+        @pl.when(hub)
         def _():
-            remote(
-                o_send.at[0, 0], o_recv.at[0, h], o_ss.at[0, 0], o_rs.at[0, h], near
-            ).wait_recv()
-
-        remote(o_send.at[0, 0], o_recv.at[1, h], o_ss.at[0, 0], o_rs.at[1, h], near).wait_recv()
+            arrived(o_recv.at[1:2, h], o_rs.at[h])
+
+        @pl.when(jnp.logical_not(hub))
+        def _():
+            arrived(o_recv.at[:, h], o_rs.at[h])
+
         (o, lse), (o_, lse_) = unpack(0, h), unpack(1, h)
         share = 1.0 / (1.0 + jnp.exp(lse_ - lse))
         o_all[...] = (o * share + o_ * (1.0 - share)).astype(BF16)
@@ -567,13 +582,6 @@
 
     q_off(0).start()
     tb_y.start()
-    for load in loads[1:]:
-        load.wait()
-    prepare_kv(mine_on(0))
-
-    @pl.when(outer)
-    def _():
-        kv_in(0).start()
 
     def queries(i, c):
         prepare_q(mine_off(i))
@@ -591,8 +599,11 @@
         return c
 
     lax.fori_loop(1, pairs, queries, 0)
+    for load in loads[7:]:
+        load.wait()
     prepare_kv(mine_off(0))
     kv_off(0).start()
+    prepare_kv(mine_on(0))
 
     def keep(i, c):
         prepare_kv(mine_off(i))
@@ -615,10 +626,7 @@
         lax.fori_loop(0, pairs, pass_queries, 0)
 
         def pass_keys(i, c):
-            @pl.when(i > 0)
-            def _():
-                kv_in(i).start()
-
+            kv_in(i).start()
             kv_off(i).wait_recv()
             kv_relay(i).start()
             return c
@@ -652,17 +660,11 @@
 
         lax.fori_loop(0, pairs, onward, 0)
         lax.fori_loop(0, pairs, onward_last, 0)
-        tb_in.wait_recv()
-        tb_y.wait_recv()
-        tb_relay.wait_recv()
+        arrived(tb.at[1:GROUP], tb_rs)
 
         def main(i, c):
-            kv_in(i).wait_recv()
-            kv_off(i).wait_recv()
-
-            for slot in (2, 3, 6, 7):
-                q_far(slot, i).wait_recv()
-            kv_relay(i).wait_recv()
+            arrived(q_held.at[0:4, i], q_rs.at[3, i])
+            arrived(held.at[:, i], kv_rs.at[i])
             order = (7, 3, 6, 2, 5, 1, 4, 0)
             top = score(order[0], i, scores_a)
             for n, slot in enumerate(order):
@@ -695,8 +697,7 @@
     for span in spans:
         acc[0, :, span] = dot(h_mine[:, :early], w[:early, span])
     w_move.wait_recv()
-    for h in range(heads - 2):
-        h_move(h).wait_recv()
+    arrived(h_recv.at[0 : heads - 2], h_rs.at[0])
     theirs = jnp.concatenate([h_recv[h] for h in range(heads - 2)], axis=1)
     for span in spans:
         acc[1, :, span] = dot(theirs, w_far[:early, span])
@@ -706,48 +707,27 @@
 
     for span in spans:
         acc[0, :, span] += dot(h_mine[:, early:], w[early:, span])
-    h_move(heads - 2).wait_recv()
-    h_move(heads - 1).wait_recv()
+    arrived(h_recv.at[heads - 2 : heads], h_rs.at[1])
     last = jnp.concatenate([h_recv[heads - 2], h_recv[heads - 1]], axis=1)
     for span in spans:
         theirs = acc[1, :, span] + dot(last, w_far[early:, span])
         mine_too = acc[0, :, span]
         out_ref[:, span] = (mine_too.astype(BF16).astype(F32) + theirs.astype(BF16).astype(F32)).astype(BF16)
 
-    def drain(i, c):
-        q_off(i).wait_send()
-        kv_off(i).wait_send()
-
-        @pl.when(inner)
-        def _():
-            for slot in (2, 3, 6, 7):
-                q_far(slot, i).wait_send()
-            for slot in range(1, HUB_SLOTS):
-                o_move(slot, i).wait_send()
-
-        @pl.when(outer)
-        def _():
-            q_in(i).wait_send()
-            kv_in(i).wait_send()
-            q_relay(i).wait_send()
-            kv_relay(i).wait_send()
-
-        return c
-
-    lax.fori_loop(0, pairs, drain, 0)
-
-    tb_y.wait_send()
+    @pl.when(inner)
+    def _():
+        left(q_held.at[0:5], q_ss)
+        left(held.at[0:1], kv_ss)
+        left(o_send, o_ss)
+        left(tb.at[0:1], tb_ss)
 
     @pl.when(outer)
     def _():
-        tb_in.wait_send()
-        tb_relay.wait_send()
-
-    def settle(h, c):
-        h_move(h).wait_send()
-        return c
-
-    lax.fori_loop(0, heads, settle, 0)
+        left(q_held.at[0:3], q_ss)
+        left(held, kv_ss)
+        left(tb.at[0:3], tb_ss)
+
+    left(h_send, h_ss)
     w_move.wait_send()
 
 
@@ -772,10 +752,9 @@
         pltpu.VMEM((heads, half, HEAD), BF16),
         pltpu.VMEM((2, half, model), F32),
         pltpu.VMEM((4, rows, HEAD), F32),
-        *[pltpu.VMEM(x.shape, BF16) for x in inputs],
-        dma((3, pairs)), dma((3, pairs)), dma((3,)), dma((3,)),
-        dma((5, pairs)), dma((HUB_SLOTS - 1, pairs)), dma((HUB_SLOTS - 1, pairs)), dma((2, heads)),
-        dma((heads,)), dma((heads,)), dma, dma, dma, dma((5,)),
+        *[pltpu.VMEM(x.shape, x.dtype) for x in inputs],
+        dma, dma((pairs,)), dma, dma, dma, dma((4, pairs)), dma, dma((heads,)), dma, dma((2,)), dma, dma, dma,
+        dma((11,)),
     ]
 
 
@@ -805,11 +784,14 @@
         slab_order, visual_q, visual_key_input, visual_v, text_k, text_v, text_mask[None], q_gain[None],
         key_norm_gain[None], jnp.asarray(lanes), jnp.asarray(perm, BF16), w_out,
     )
-    if n == 2 * GROUP and rows % HEAD == 0 and heads % 2 == 0:
+    if n == 2 * GROUP and rows % HEAD == 0 and heads % 2 == 0 and heads > 3:
         run = functools.partial(hub_kernel, chunks)
-        scratch = hub_scratch(rows, trows, heads, model, w_out.shape, operands[1:6])
+        operands = (slab_order[None],) + operands[1:]
+        scratch = hub_scratch(rows, trows, heads, model, w_out.shape, operands[1:6] + operands[:1] + operands[6:11])
+        places = [anywhere] * 12
     else:
         run = functools.partial(kernel, n, chunks)
+        places = [pl.BlockSpec(memory_space=pltpu.SMEM)] + [anywhere] * 5 + [vm] * 5 + [anywhere]
         scratch = [
                 pltpu.VMEM((GROUP, heads, 2 * keys, HEAD), BF16),
                 pltpu.VMEM((GROUP, trows, HEAD), BF16),
@@ -834,7 +816,7 @@
     return pl.pallas_call(
         run,
         out_shape=pltpu.VMEM((half, model), BF16),
-        in_specs=[pl.BlockSpec(memory_space=pltpu.SMEM)] + [anywhere] * 5 + [vm] * 5 + [anywhere],
+        in_specs=places,
         out_specs=vm,
         scratch_shapes=scratch,
         compiler_params=pltpu.CompilerParams(

time: 47.3 us -> 45.7 us (0.966)
  Pallas kernels: 45.6 us -> 44 us
    pallas_call x1, Pallas kernels: 45.6 us -> 44 us  [body(): pl.pallas_call(run, out_shape=pltpu.VMEM((half, model), BF16), in_specs=p...]
where the time goes in v2:
time: 45.7 us; the launch traced here: 45.5 us
  Pallas kernels  44 us (96%)
  local copies, waits for them, and re-layouts  0.88 us (2%)
  between operations  0.66 us (1%)
    pallas_call x1, Pallas kernels, body(): pl.pallas_call(run, out_shape=pltpu.VMEM((half, model), BF16), in_specs=p...  44 us

profile of v2, /device:TPU:1, one launch (start us, length us, event | category | flops | bytes accessed | tf_op | source)
XLA Modules:
  0.0 45.5 jit_solution(5116449795146511110)
XLA Ops:
  0.7 44.0 %shard_map.118 = bf16[128,3072]{1,0:T(8,128)(2,1)S(1)} custom-call(s32[1,1]{1,0:T(1,128)} %bitcast.4.slab_hbm, bf16[256,768]{1,0:T(8,128)(2,1)} %q_hbm.1, bf16[256,768]{1,0:T(8,128)(2,1)} %k_hbm.1, bf16[256,768]{1,0:T(8,128)(2,1)} %v_hbm.1, bf16[32,768]{1,0:T(8,128)(2,1)} %tk_hbm.1, bf16[32,768]{1,0:T(8,128)(2,1)} %tv_hbm.1, s32[1,32]{1,0:T(1,128)} %bitcast.5, ...), custom_call_target="tpu_custom_call" | custom-call | tf_op jit(solution)/shard_map/pallas_call | solution.py:816
  44.6 0.9 %copy.14 = bf16[128,3072]{1,0:T(8,128)(2,1)} copy(bf16[128,3072]{1,0:T(8,128)(2,1)S(1)} %shard_map.118) | data formatting | bytes 1572864

commit v3 on v2

--- a/solution.py
+++ b/solution.py
@@ -665,7 +665,7 @@
         def main(i, c):
             arrived(q_held.at[0:4, i], q_rs.at[3, i])
             arrived(held.at[:, i], kv_rs.at[i])
-            order = (7, 3, 6, 2, 5, 1, 4, 0)
+            order = (7, 5, 3, 1, 6, 2, 4, 0)
             top = score(order[0], i, scores_a)
             for n, slot in enumerate(order):
                 here, there = ((scores_a, scores_b), (scores_b, scores_a))[n % 2]

time: 45.7 us -> 44.5 us (0.974)
  Pallas kernels: 44 us -> 42.8 us
    pallas_call x1, Pallas kernels: 44 us -> 42.8 us  [body(): pl.pallas_call(run, out_shape=pltpu.VMEM((half, model), BF16), in_specs=p...]
where the time goes in v3:
time: 44.5 us; the launch traced here: 44.4 us
  Pallas kernels  42.8 us (96%)
  local copies, waits for them, and re-layouts  0.88 us (2%)
  between operations  0.66 us (1%)
    pallas_call x1, Pallas kernels, body(): pl.pallas_call(run, out_shape=pltpu.VMEM((half, model), BF16), in_specs=p...  42.8 us

profile of v3, /device:TPU:1, one launch (start us, length us, event | category | flops | bytes accessed | tf_op | source)
XLA Modules:
  0.0 44.4 jit_solution(6560713447632581282)
XLA Ops:
  0.7 42.8 %shard_map.118 = bf16[128,3072]{1,0:T(8,128)(2,1)S(1)} custom-call(s32[1,1]{1,0:T(1,128)} %bitcast.4.slab_hbm, bf16[256,768]{1,0:T(8,128)(2,1)} %q_hbm.1, bf16[256,768]{1,0:T(8,128)(2,1)} %k_hbm.1, bf16[256,768]{1,0:T(8,128)(2,1)} %v_hbm.1, bf16[32,768]{1,0:T(8,128)(2,1)} %tk_hbm.1, bf16[32,768]{1,0:T(8,128)(2,1)} %tv_hbm.1, s32[1,32]{1,0:T(1,128)} %bitcast.5, ...), custom_call_target="tpu_custom_call" | custom-call | tf_op jit(solution)/shard_map/pallas_call | solution.py:816
  43.5 0.9 %copy.14 = bf16[128,3072]{1,0:T(8,128)(2,1)} copy(bf16[128,3072]{1,0:T(8,128)(2,1)S(1)} %shard_map.118) | data formatting | bytes 1572864

commit v4 on v3

--- a/solution.py
+++ b/solution.py
@@ -623,43 +623,475 @@
             q_relay(i).start()
             return c
 
-        lax.fori_loop(0, pairs, pass_queries, 0)
-
         def pass_keys(i, c):
             kv_in(i).start()
             kv_off(i).wait_recv()
             kv_relay(i).start()
             return c
 
-        lax.fori_loop(0, pairs, pass_keys, 0)
+        lax.fori_loop(0, 1, pass_queries, 0)
+        pass_keys(0, 0)
+        lax.fori_loop(1, pairs, pass_queries, 0)
+        lax.fori_loop(1, pairs, pass_keys, 0)
 
     w_copy.wait()
     w_move.start()
+    half = rows // 2
+
+    def attend(j, h):
+        queries = qs[j, h]
+        scores = []
+        top = None
+        for slot in range(GROUP):
+            sc = nt(kv[slot, h, 0:keys, :], queries)
+            mark = tb[slot].astype(F32)
+            mark = jnp.concatenate([mark] * (rows // HEAD), axis=1)
+            sc = jnp.concatenate([sc[0:rows], sc[rows:keys] + mark], axis=0)
+            peak = jnp.max(sc, axis=0, keepdims=True)
+            top = peak if top is None else jnp.maximum(top, peak)
+            scores.append(sc)
+        total = None
+        acc = None
+        for slot in range(GROUP):
+            p = jnp.exp(scores[slot] - top)
+            part = jnp.sum(p, axis=0, keepdims=True)
+            mixed = tn(kv[slot, h, keys : 2 * keys, :], p.astype(BF16))
+            total = part if total is None else total + part
+            acc = mixed if acc is None else acc + mixed
+        return acc / total, top + jnp.log(total)
+
+    def main(h, c):
+        @pl.when(h + 1 < heads)
+        def _():
+            kv_z(h + 1).wait_recv()
+            kv_relay(h + 1).start()
+
+        send(h, True)
+
+        kv_y(h).wait_recv()
+
+        @pl.when(h == 0)
+        def _():
+            tb_y.wait_recv()
+            tb_relay.wait_recv()
+
+        for j in range(1, a):
+            q_move(j, h).wait_recv()
+        kv_relay(h).wait_recv()
+        for j in range(1, a):
+            o, lse = attend(j, h)
+            high = lse.astype(BF16)
+            rest = lse - high.astype(F32)
+            mid = rest.astype(BF16)
+            tail = (rest - mid.astype(F32)).astype(BF16)
+            o_send[j - 1, h, HEAD : HEAD + 16, :] = jnp.concatenate(
+                [high.astype(F32), mid.astype(F32), tail.astype(F32), jnp.zeros((13, rows), F32)], axis=0
+            ).astype(BF16)
+            o_send[j - 1, h, 0:HEAD, :] = o.astype(BF16)
+            o_move(j, h).start()
+        o, lse = attend(0, h)
+        o_own[h] = o
+        lse_own[h] = jnp.broadcast_to(lse, (8, rows))
+
+        @pl.when(h > 0)
+        def _():
+            merge(h - 1)
+
+        return c
+
+    def merge(h):
+        lses = [lse_own[h][0:1]]
+        parts = [o_own[h]]
+        for j in range(1, a):
+            o_move(j, h).wait_recv()
+            stats = o_recv[j - 1, h, HEAD : HEAD + 16, :].astype(F32)
+            lses.append(stats[0:1] + stats[1:2] + stats[2:3])
+            parts.append(o_recv[j - 1, h, 0:HEAD, :].astype(F32))
+        top = functools.reduce(jnp.maximum, lses)
+        shares = [jnp.exp(x - top) for x in lses]
+        total = functools.reduce(jnp.add, shares)
+        o = functools.reduce(jnp.add, [x * y for x, y in zip(parts, shares)]) / total
+        o_all[...] = o.astype(BF16)
+        h_send[h] = o_all[:, pl.ds(pl.multiple_of((1 - t) * half, half), half)].T
+        h_move(h).start()
+        cols = pl.ds(pl.multiple_of(h * HEAD, HEAD), HEAD)
+        h_mine[:, cols] = o_all[:, pl.ds(pl.multiple_of(t * half, half), half)].T
+
+    lax.fori_loop(0, heads, main, 0)
+
+    step = w.shape[1] // chunks
+    spans = [slice(i * step, (i + 1) * step) for i in range(chunks)]
+    early = (heads - 1) * HEAD
+
+    def dot(x, y):
+        return jnp.dot(x, y, preferred_element_type=F32)
+
+    for span in spans:
+        acc[0, :, span] = dot(h_mine[:, :early], w[:early, span])
+    w_move.wait_recv()
+    for h in range(heads - 1):
+        h_move(h).wait_recv()
+    theirs = jnp.concatenate([h_recv[h] for h in range(heads - 1)], axis=1)
+    for span in spans:
+        acc[1, :, span] = dot(theirs, w_far[:early, span])
+    merge(heads - 1)
+    for span in spans:
+        acc[0, :, span] += dot(h_mine[:, early:], w[early:, span])
+    h_move(heads - 1).wait_recv()
+    for span in spans:
+        far = acc[1, :, span] + dot(h_recv[heads - 1], w_far[early:, span])
+        near = acc[0, :, span]
+        out_ref[:, span] = (near.astype(BF16).astype(F32) + far.astype(BF16).astype(F32)).astype(BF16)
+
+    def drain(h, c):
+        kv_z(h).wait_send()
+        kv_y(h).wait_send()
+        kv_relay(h).wait_send()
+        h_move(h).wait_send()
+        for j in range(1, a):
+            q_move(j, h).wait_send()
+            o_move(j, h).wait_send()
+        return c
+
+    lax.fori_loop(0, heads, drain, 0)
+    tb_z.wait_send()
+    tb_y.wait_send()
+    tb_relay.wait_send()
+    w_move.wait_send()
+
+
+def hub_kernel(
+    chunks,
+    slab_hbm, q_hbm, k_hbm, v_hbm, tk_hbm, tv_hbm, mask_hbm, qg_hbm, kg_hbm, lanes_hbm, perm_hbm, w_ref,
+    out_ref,
+    mine, held, tb, q_mine, q_held, o_send, o_recv, scores_a, scores_b, o_all, w, w_far, h_mine, h_send, h_recv,
+    acc, tabs, q_ref, k_ref, v_ref, tk_ref, tv_ref, slab_ref, mask_ref, qg_ref, kg_ref, lanes_ref, perm_ref,
+    kv_ss, kv_rs, tb_ss, tb_rs, q_ss, q_rs, o_ss, o_rs, h_ss, h_rs, wf_ss, wf_rs, w_sem, in_sem,
+):
+    rows, width = q_ref.shape
+    heads = width // HEAD
+    trows = tk_ref.shape[0]
+    keys = rows + trows
+    half = rows // 2
+    pairs = heads // 2
+    g, s, t = lax.axis_index("grp"), lax.axis_index("seq"), lax.axis_index("tp")
+    u, low = s // GROUP, s % GROUP
+    row, col = low // 2, low % 2
+    inner = row + u == 1
+    outer = row + u != 1
+    aside = 1 - 2 * col
+
+    def dev(seq):
+        return (g, seq, t)
+
+    near_s, far_s, cross_s = s + 2 - 4 * row, s + 2 - 4 * u, s + GROUP - 2 * GROUP * u
+    near, far, cross, ydev = dev(near_s), dev(far_s), dev(cross_s), dev(s + aside)
+    near_y, far_y, cross_y = dev(near_s + aside), dev(far_s + aside), dev(cross_s + aside)
+    tdev = (g, s, 1 - t)
+
+    barrier = pltpu.get_barrier_semaphore()
+    friends = [near, ydev, tdev]
+    for friend in friends:
+        pl.semaphore_signal(barrier, inc=1, device_id=friend, device_id_type=MESH)
+
+    @pl.when(inner)
+    def _():
+        pl.semaphore_signal(barrier, inc=1, device_id=far, device_id_type=MESH)
+
+    loads = [
+        pltpu.make_async_copy(x, y, in_sem.at[i])
+        for i, (x, y) in enumerate(
+            (
+                (q_hbm, q_ref), (lanes_hbm, lanes_ref), (slab_hbm, slab_ref), (qg_hbm, qg_ref), (kg_hbm, kg_ref),
+                (perm_hbm, perm_ref), (mask_hbm, mask_ref),
+                (k_hbm, k_ref), (tk_hbm, tk_ref), (v_hbm, v_ref), (tv_hbm, tv_ref),
+            )
+        )
+    ]
+    for load in loads:
+        load.start()
+    w_copy = pltpu.make_async_copy(w_ref, w, w_sem)
+    w_copy.start()
+
+    def remote(src, dst, ss, rs, to):
+        return pltpu.make_async_remote_copy(
+            src_ref=src, dst_ref=dst, send_sem=ss, recv_sem=rs, device_id=to, device_id_type=MESH
+        )
+
+    def mine_on(i):
+        return 2 * i + col
+
+    def mine_off(i):
+        return 2 * i + 1 - col
+
+    def kv_move(src, slot, i, to):
+        return remote(src, held.at[slot - 1, i], kv_ss, kv_rs.at[i], to)
+
+    def kv_in(i):
+        return kv_move(mine.at[mine_on(i)], 1, i, near)
+
+    def kv_off(i):
+        return kv_move(mine.at[mine_off(i)], 2, i, ydev)
+
+    def kv_relay(i):
+        return kv_move(held.at[1, i], 3, i, near)
+
+    def q_move(src, slot, i, to):
+        return remote(src, q_held.at[slot - 1, i], q_ss, q_rs.at[{1: 0, 4: 1, 5: 2}.get(slot, 3), i], to)
+
+    def q_in(i):
+        return q_move(q_mine.at[mine_on(i)], 1, i, near)
+
+    def q_off(i):
+        return q_move(q_mine.at[mine_off(i)], 4, i, ydev)
+
+    def q_relay(i):
+        return q_move(q_held.at[3, i], 5, i, near)
+
+    def q_far(slot, i):
+        if slot == 2:
+            return q_move(q_mine.at[mine_on(i)], 2, i, far)
+        start = {3: 1, 6: 4, 7: 5}[slot]
+        return q_move(q_held.at[start - 1, i], slot, i, far)
+
+    def o_move(slot, i):
+        index, to = {
+            1: (0, near), 4: (0, ydev), 5: (0, near_y),
+            2: (1, far), 3: (1, cross), 6: (1, far_y), 7: (1, cross_y),
+        }[slot]
+        h = mine_on(i)
+        return remote(
+            o_send.at[slot - 1, i], o_recv.at[index, h], o_ss, o_rs.at[h], to
+        )
+
+    def h_move(h):
+        return remote(h_send.at[h], h_recv.at[h], h_ss, h_rs.at[h // (heads - 2)], tdev)
+
+    def arrived(ref, sem):
+        remote(ref, ref, sem, sem, near).wait_recv()
+
+    def left(ref, sem):
+        remote(ref, ref, sem, sem, near).wait_send()
+
+    w_move = remote(w, w_far, wf_ss, wf_rs, tdev)
+    tb_in = remote(tb.at[0], tb.at[1], tb_ss, tb_rs, near)
+    tb_y = remote(tb.at[0], tb.at[2], tb_ss, tb_rs, ydev)
+    tb_relay = remote(tb.at[2], tb.at[3], tb_ss, tb_rs, near)
+
+    for load in loads[1:7]:
+        load.wait()
+    freq, part, lead = lanes_ref[0:1, :], lanes_ref[1:2, :], lanes_ref[2:3, :]
+    blocks = rows // WIDE
+    block = lax.broadcasted_iota(jnp.int32, (blocks, HEAD), 0)
+    slab = slab_ref[...] * SLAB_H
+    place = jnp.where(part < 0.5, (block // SLAB_H).astype(F32), (slab + block % SLAB_H).astype(F32)) * freq
+    across = lax.broadcasted_iota(jnp.int32, (WIDE, HEAD), 0).astype(F32) * freq
+    trig = (jnp.cos(place), jnp.cos(across)), (jnp.sin(place), jnp.sin(across))
+
+    def partner(x):
+        wide = jnp.broadcast_to(x, (8, HEAD))
+        near, far = PARTS[0] // 2, PARTS[1] // 2
+        after = jnp.where(part < 0.5, pltpu.roll(wide, HEAD - near, 1), pltpu.roll(wide, HEAD - far, 1))
+        before = jnp.where(part < 0.5, pltpu.roll(wide, near, 1), pltpu.roll(wide, far, 1))
+        return jnp.where(lead > 0.5, after, before)[0:1]
+
+    scale_q = F32(1.0) / jnp.sqrt(F32(HEAD))
+    kg = kg_ref[...]
+    qg = qg_ref[...] * scale_q
+    for which, (by_block, by_column) in enumerate(trig):
+        for gain, index in ((qg, 0), (kg, 2)):
+            gain = gain if which == 0 else partner(gain)
+            for i in range(blocks):
+                full = jnp.where(part < 1.5, by_block[i : i + 1], by_column)
+                tabs[index + which, i * WIDE : (i + 1) * WIDE, :] = full * gain
+    line = lax.broadcasted_iota(jnp.int32, (trows, trows), 0)
+    lane = lax.broadcasted_iota(jnp.int32, (trows, trows), 1)
+    mark = jnp.where((line == lane) & (mask_ref[...] != 1), F32(NEGATIVE), F32(0.0))
+    tb[0] = jnp.broadcast_to(jnp.sum(mark, axis=1, keepdims=True), (trows, HEAD)).astype(BF16)
+
+    def norm_scale(x32):
+        return lax.rsqrt(jnp.mean(x32 * x32, axis=-1, keepdims=True) + 0.05)
+
+    def rotated(x, which):
+        x32 = x.astype(F32)
+        turned = jnp.dot(x, perm_ref[...], preferred_element_type=F32)
+        return ((x32 * tabs[which] + turned * tabs[which + 1]) * norm_scale(x32)).astype(BF16)
+
+    def prepare_q(h):
+        q_mine[h] = rotated(q_ref[:, pl.ds(pl.multiple_of(h * HEAD, HEAD), HEAD)], 0)
+
+    def prepare_kv(h):
+        cols = pl.ds(pl.multiple_of(h * HEAD, HEAD), HEAD)
+        mine[h, 0:rows, :] = rotated(k_ref[:, cols], 2)
+        tk = tk_ref[:, cols].astype(F32)
+        mine[h, rows:keys, :] = (tk * norm_scale(tk) * kg).astype(BF16)
+        mine[h, keys : keys + rows, :] = v_ref[:, cols]
+        mine[h, keys + rows : 2 * keys, :] = tv_ref[:, cols]
+
+    def side(slot, i, part):
+        where = pl.ds(part * keys, keys)
+        return held[slot - 1, i, where, :] if slot else mine[mine_on(i), where, :]
+
+    def score(slot, i, where):
+        queries = q_held[slot - 1, i] if slot else q_mine[mine_on(i)]
+        top = None
+        for n in range(GROUP):
+            sc = nt(side(n, i, 0), queries)
+            mark = tb[n].astype(F32)
+            mark = jnp.concatenate([mark] * (rows // HEAD), axis=1)
+            sc = jnp.concatenate([sc[0:rows], sc[rows:keys] + mark], axis=0)
+            where[n] = sc
+            peak = jnp.max(sc, axis=0, keepdims=True)
+            top = peak if top is None else jnp.maximum(top, peak)
+        return top
+
+    def weigh(i, where, top):
+        total = None
+        mixed = None
+        for n in range(GROUP):
+            p = jnp.exp(where[n] - top)
+            amount = jnp.sum(p, axis=0, keepdims=True)
+            got = tn(side(n, i, 1), p.astype(BF16))
+            total = amount if total is None else total + amount
+            mixed = got if mixed is None else mixed + got
+        return mixed / total, top + jnp.log(total)
+
+    wides = rows // HEAD
+
+    def pack(to, o, lse):
+        high = lse.astype(BF16).astype(F32)
+        rest = lse - high
+        mid = rest.astype(BF16).astype(F32)
+        pieces = [x[:, i * HEAD : (i + 1) * HEAD] for x in (high, mid, rest - mid) for i in range(wides)]
+        pieces.append(jnp.zeros((STATS - 3 * wides, HEAD), F32))
+        to[rows : rows + STATS, :] = jnp.concatenate(pieces, axis=0).astype(BF16)
+        for i in range(wides):
+            to[i * HEAD : (i + 1) * HEAD, :] = o[:, i * HEAD : (i + 1) * HEAD].astype(BF16)
+
+    def unpack(index, h):
+        o = jnp.concatenate([o_recv[index, h, i * HEAD : (i + 1) * HEAD, :] for i in range(wides)], axis=1)
+        stats = o_recv[index, h, rows : rows + STATS, :].astype(F32)
+        levels = [
+            jnp.concatenate([stats[k * wides + i : k * wides + i + 1] for i in range(wides)], axis=1)
+            for k in range(3)
+        ]
+        return o.astype(F32), levels[0] + levels[1] + levels[2]
+
+    def merge(h):
+        hub = jnp.logical_and(inner, h % 2 == col)
+
+        @pl.when(hub)
+        def _():
+            arrived(o_recv.at[1:2, h], o_rs.at[h])
+
+        @pl.when(jnp.logical_not(hub))
+        def _():
+            arrived(o_recv.at[:, h], o_rs.at[h])
+
+        (o, lse), (o_, lse_) = unpack(0, h), unpack(1, h)
+        share = 1.0 / (1.0 + jnp.exp(lse_ - lse))
+        o_all[...] = (o * share + o_ * (1.0 - share)).astype(BF16)
+        h_send[h] = o_all[:, pl.ds(pl.multiple_of((1 - t) * half, half), half)].T
+        h_move(h).start()
+        cols = pl.ds(pl.multiple_of(h * HEAD, HEAD), HEAD)
+        h_mine[:, cols] = o_all[:, pl.ds(pl.multiple_of(t * half, half), half)].T
+
+    loads[0].wait()
+    prepare_q(mine_off(0))
+    prepare_q(mine_on(0))
+
+    @pl.when(inner)
+    def _():
+        pl.semaphore_wait(barrier, len(friends) + 1)
+        q_far(2, 0).start()
 
     @pl.when(outer)
     def _():
-        def collect(h, c):
-            merge(h)
+        pl.semaphore_wait(barrier, len(friends))
+        q_in(0).start()
+        tb_in.start()
+
+    q_off(0).start()
+    tb_y.start()
+
+    def queries(i, c):
+        prepare_q(mine_off(i))
+        q_off(i).start()
+        prepare_q(mine_on(i))
+
+        @pl.when(inner)
+        def _():
+            q_far(2, i).start()
+
+        @pl.when(outer)
+        def _():
+            q_in(i).start()
+
+        return c
+
+    lax.fori_loop(1, pairs, queries, 0)
+    for load in loads[7:]:
+        load.wait()
+    prepare_kv(mine_off(0))
+    kv_off(0).start()
+    prepare_kv(mine_on(0))
+
+    def keep(i, c):
+        prepare_kv(mine_off(i))
+        kv_off(i).start()
+        prepare_kv(mine_on(i))
+        return c
+
+    lax.fori_loop(1, pairs, keep, 0)
+
+    @pl.when(outer)
+    def _():
+        tb_y.wait_recv()
+        tb_relay.start()
+
+        def pass_queries(i, c):
+            q_off(i).wait_recv()
+            q_relay(i).start()
             return c
 
-        lax.fori_loop(0, heads - 2, collect, 0)
+        lax.fori_loop(0, pairs, pass_queries, 0)
+
+        def pass_keys(i, c):
+            kv_in(i).start()
+            kv_off(i).wait_recv()
+            kv_relay(i).start()
+            return c
+
+        lax.fori_loop(0, pairs, pass_keys, 0)
+
+    w_copy.wait()
+    w_move.start()
 
     @pl.when(inner)
     def _():
-        def onward(i, c):
+        def onward(i):
             q_in(i).wait_recv()
             q_far(3, i).start()
             q_off(i).wait_recv()
             q_far(6, i).start()
-            return c
-
-        def onward_last(i, c):
+
+        def onward_last(i):
             q_relay(i).wait_recv()
             q_far(7, i).start()
+
+        onward(0)
+        onward(1)
+
+        def trail(i, c):
+            onward_last(i)
+
+            @pl.when(i + 2 < pairs)
+            def _():
+                onward(i + 2)
+
             return c
 
-        lax.fori_loop(0, pairs, onward, 0)
-        lax.fori_loop(0, pairs, onward_last, 0)
+        lax.fori_loop(0, pairs, trail, 0)
         arrived(tb.at[1:GROUP], tb_rs)
 
         def main(i, c):
@@ -678,14 +1110,15 @@
                 else:
                     pack(o_recv.at[0, mine_on(i)], o, lse)
 
-            @pl.when(i > 0)
-            def _():
-                merge(2 * i - 2)
-                merge(2 * i - 1)
-
             return c
 
         lax.fori_loop(0, pairs, main, 0)
+
+    def collect(h, c):
+        merge(h)
+        return c
+
+    lax.fori_loop(0, heads - 2, collect, 0)
 
     step = w.shape[1] // chunks
     spans = [slice(i * step, (i + 1) * step) for i in range(chunks)]

time: 44.5 us -> 44.4 us (level)
  no operation moved by 1% of the time
where the time goes in v4:
time: 44.4 us; the launch traced here: 44.2 us
  Pallas kernels  42.6 us (96%)
  local copies, waits for them, and re-layouts  0.88 us (2%)
  between operations  0.66 us (1%)
    pallas_call x1, Pallas kernels, body(): pl.pallas_call(run, out_shape=pltpu.VMEM((half, model), BF16), in_specs=p...  42.6 us

profile of v4, /device:TPU:1, one launch (start us, length us, event | category | flops | bytes accessed | tf_op | source)
XLA Modules:
  0.0 44.2 jit_solution(6675940805730477465)
XLA Ops:
  0.7 42.6 %shard_map.118 = bf16[128,3072]{1,0:T(8,128)(2,1)S(1)} custom-call(s32[1,1]{1,0:T(1,128)} %bitcast.4.slab_hbm, bf16[256,768]{1,0:T(8,128)(2,1)} %q_hbm.1, bf16[256,768]{1,0:T(8,128)(2,1)} %k_hbm.1, bf16[256,768]{1,0:T(8,128)(2,1)} %v_hbm.1, bf16[32,768]{1,0:T(8,128)(2,1)} %tk_hbm.1, bf16[32,768]{1,0:T(8,128)(2,1)} %tv_hbm.1, s32[1,32]{1,0:T(1,128)} %bitcast.5, ...), custom_call_target="tpu_custom_call" | custom-call | tf_op jit(solution)/shard_map/pallas_call | solution.py:1249
  43.3 0.9 %copy.14 = bf16[128,3072]{1,0:T(8,128)(2,1)} copy(bf16[128,3072]{1,0:T(8,128)(2,1)S(1)} %shard_map.118) | data formatting | bytes 1572864

commit v5 on v4

--- a/solution.py
+++ b/solution.py
@@ -1094,10 +1094,7 @@
         lax.fori_loop(0, pairs, trail, 0)
         arrived(tb.at[1:GROUP], tb_rs)
 
-        def main(i, c):
-            arrived(q_held.at[0:4, i], q_rs.at[3, i])
-            arrived(held.at[:, i], kv_rs.at[i])
-            order = (7, 5, 3, 1, 6, 2, 4, 0)
+        def serve(i, order):
             top = score(order[0], i, scores_a)
             for n, slot in enumerate(order):
                 here, there = ((scores_a, scores_b), (scores_b, scores_a))[n % 2]
@@ -1109,6 +1106,17 @@
                     o_move(slot, i).start()
                 else:
                     pack(o_recv.at[0, mine_on(i)], o, lse)
+
+        def main(i, c):
+            arrived(q_held.at[0:4, i], q_rs.at[3, i])
+            arrived(held.at[:, i], kv_rs.at[i])
+            @pl.when(t == 0)
+            def _():
+                serve(i, (7, 3, 5, 6, 2, 1, 4, 0))
+
+            @pl.when(t == 1)
+            def _():
+                serve(i, (5, 7, 1, 3, 4, 6, 2, 0))
 
             return c
 

time: 44.4 us -> 44.7 us (level)
  no operation moved by 1% of the time
where the time goes in v5:
time: 44.7 us; the launch traced here: 44.6 us
  Pallas kernels  43 us (96%)
  local copies, waits for them, and re-layouts  0.88 us (2%)
  between operations  0.66 us (1%)
    pallas_call x1, Pallas kernels, body(): pl.pallas_call(run, out_shape=pltpu.VMEM((half, model), BF16), in_specs=p...  43 us

profile of v5, /device:TPU:1, one launch (start us, length us, event | category | flops | bytes accessed | tf_op | source)
XLA Modules:
  0.0 44.6 jit_solution(1669742191491994460)
XLA Ops:
  0.7 43.0 %shard_map.118 = bf16[128,3072]{1,0:T(8,128)(2,1)S(1)} custom-call(s32[1,1]{1,0:T(1,128)} %bitcast.4.slab_hbm, bf16[256,768]{1,0:T(8,128)(2,1)} %q_hbm.1, bf16[256,768]{1,0:T(8,128)(2,1)} %k_hbm.1, bf16[256,768]{1,0:T(8,128)(2,1)} %v_hbm.1, bf16[32,768]{1,0:T(8,128)(2,1)} %tk_hbm.1, bf16[32,768]{1,0:T(8,128)(2,1)} %tv_hbm.1, s32[1,32]{1,0:T(1,128)} %bitcast.5, ...), custom_call_target="tpu_custom_call" | custom-call | tf_op jit(solution)/shard_map/pallas_call | solution.py:1257
  43.7 0.9 %copy.14 = bf16[128,3072]{1,0:T(8,128)(2,1)} copy(bf16[128,3072]{1,0:T(8,128)(2,1)S(1)} %shard_map.118) | data formatting | bytes 1572864
